TPU v7x, 32 devices: a whole 2x2x4 slice. The times are simulated.
32 devices in a mesh: member: 2 (over x), node: 16 (over z, y, core).
Axes of the slice: x: 2, y: 2, z: 4, core: 2. Of those that a mesh axis runs over, the one named last changes fastest.
Arguments:
- latent: bfloat16 [4, 4096, 512], P('member', 'node'), may hold values from -6 to 6
- noise_draw: float32 [4, 32], P('member'), may hold values from -4 to 4
- mesh_links: int32 [6, 4096], P(None, 'node'), may hold values from 0 to 4095, as said below
- w_cond: float32 [2, 32, 512], replicated, may hold values from -0.3 to 0.3
- w_in: bfloat16 [2, 1024, 512], replicated, may hold values from -0.1875 to 0.1875
- w_out: bfloat16 [2, 512, 512], replicated, may hold values from -0.25 to 0.25
- dec_gain: float32 [512], replicated, may hold values from 0.5 to 1.5
- w_dec: bfloat16 [83, 512], replicated, may hold values from -2 to 2
- target_vertex_map: int32 [16384], P('node'), may hold values from 0 to 4095, as said below
- prior_field: bfloat16 [83, 16384], P(None, 'node'), may hold values from -6 to 6
- target: bfloat16 [83, 16384], P(None, 'node'), may hold values from -6 to 6
- location_loss_factor: float32 [16384], P('node'), may hold values from 8 to 24
Outputs:
- prediction_sensitivity: bfloat16 [4, 83, 16384], P('member', None, 'node')
- vertex_attribute_sensitivity: bfloat16 [4, 4096, 512], P('member', 'node')
Inputs may be any that keep to these rules, and one draw needn't show every extreme that they name: mesh_links[k, n] = (n + s) mod 4096 with 1 <= |s| <= 96: every neighbour of a node lies within 96 positions of it along the node order, counted around the end. target_vertex_map[g] // 256 == g // 1024.
All inputs are finite; a program needn't handle non-finite values.
Results may differ from a plain program's by a relative error of at most 0.007.
Values may be sent and summed in bfloat16 or wider, within the bound.
A program may use at most 64 MiB of HBM per device.

v0:
```python
import jax
import jax.numpy as jnp
from jax import lax
from jax.sharding import PartitionSpec as P

WIN = 96


NORM_EPS = 1e-06
DIST_EPS = 1e-06


def extended(cells, sides, width):
    for axis, dim in sides:
        count = lax.axis_size(axis)
        head = lax.slice_in_dim(cells, 0, width, axis=dim)
        tail = lax.slice_in_dim(cells, cells.shape[dim] - width, cells.shape[dim], axis=dim)
        cells = jnp.concatenate(
            [
                lax.ppermute(tail, axis, [(i, (i + 1) % count) for i in range(count)]),
                cells,
                lax.ppermute(head, axis, [((i + 1) % count, i) for i in range(count)]),
            ],
            axis=dim,
        )
    return cells


def apply_layer_norm(values, scaling):
    inverse = lax.rsqrt(jnp.mean(values * values, axis=-1, keepdims=True) + NORM_EPS)
    return (values * inverse * scaling).astype(jnp.bfloat16)


def neighbour_mean(normalized_rows, mesh_links, first_row, node_total, margin):
    inner_rows = mesh_links.shape[1]
    positions = jnp.arange(inner_rows, dtype=jnp.int32)
    own_global = first_row + margin + positions
    summed = jnp.zeros(
        (normalized_rows.shape[0], inner_rows, normalized_rows.shape[2]), jnp.float32
    )
    for slot_index in range(mesh_links.shape[0]):
        offsets = jnp.mod(mesh_links[slot_index] - own_global + margin, node_total) - margin
        summed = summed + jnp.take(normalized_rows, margin + positions + offsets, axis=1).astype(
            jnp.float32
        )
    return (summed / mesh_links.shape[0]).astype(jnp.bfloat16)


def layer_update(normed_rows, neighbours, w_in_layer, w_out_layer):
    joined = jnp.concatenate([normed_rows, neighbours], axis=2)
    preact = jnp.einsum("mrk,kl->mrl", joined, w_in_layer, preferred_element_type=jnp.float32)
    activated = jax.nn.silu(preact).astype(jnp.bfloat16)
    return jnp.einsum("mrk,kl->mrl", activated, w_out_layer, preferred_element_type=jnp.float32)


def pull_total(anchors, others, initial):

    def add_pull(carried, other_member):
        offset = anchors - other_member.astype(jnp.float32)[None]
        spread = jnp.sqrt(jnp.sum(offset * offset, axis=1, keepdims=True) + DIST_EPS)
        return (carried + offset / spread, None)

    return lax.scan(add_pull, initial, others)[0]


def score_grad(anchors, pull_sums, truth_rows, weights, ensemble):
    missed = anchors - truth_rows.astype(jnp.float32)[None]
    reached = jnp.sqrt(jnp.sum(missed * missed, axis=1, keepdims=True) + DIST_EPS)
    skill_measures = missed / (ensemble * reached) - pull_sums / (ensemble * (ensemble - 1))
    return (weights[None, None, :] * skill_measures).astype(jnp.bfloat16)


def per_device(
    latent,
    noise_draw,
    mesh_links,
    w_cond,
    w_in,
    w_out,
    dec_gain,
    w_dec,
    target_vertex_map,
    prior_field,
    target,
    location_loss_factor,
):
    local_ensemble_slice = latent.shape[0]
    node_rows = latent.shape[1]
    node_total = node_rows * lax.axis_size("node")
    first_node = lax.axis_index("node") * node_rows
    reach_rows = WIN
    layer_count = w_in.shape[0]
    noise_scale_factors = [
        (1.0 + jnp.dot(noise_draw, w_cond[current_layer_index], precision=lax.Precision.HIGHEST))[
            :, None, :
        ]
        for current_layer_index in range(layer_count)
    ]
    processor_state = latent.astype(jnp.float32)
    for current_layer_index in range(layer_count):
        normalized_rows = apply_layer_norm(
            processor_state, noise_scale_factors[current_layer_index]
        )
        widened = extended(normalized_rows, (("node", 1),), reach_rows)
        neighbours = neighbour_mean(
            widened, mesh_links, first_node - reach_rows, node_total, reach_rows
        )
        processor_state = processor_state + layer_update(
            normalized_rows, neighbours, w_in[current_layer_index], w_out[current_layer_index]
        )
    features = apply_layer_norm(processor_state, dec_gain)
    readout_result = jnp.einsum("cl,mnl->mcn", w_dec, features, preferred_element_type=jnp.float32)
    local_assign = target_vertex_map - first_node
    ensemble_prediction = (
        prior_field.astype(jnp.float32)[None] + jnp.take(readout_result, local_assign, axis=2)
    ).astype(jnp.bfloat16)
    variable_total = ensemble_prediction.shape[1]
    location_entries = ensemble_prediction.shape[2]
    member_group_lists = lax.axis_size("member")
    ensemble = local_ensemble_slice * member_group_lists
    section_rows = location_entries // member_group_lists
    partition_pieces = ensemble_prediction.reshape(
        local_ensemble_slice, variable_total, member_group_lists, section_rows
    )
    regrouped = lax.all_to_all(
        partition_pieces, "member", split_axis=2, concat_axis=0, tiled=True
    ).reshape(ensemble, variable_total, section_rows)
    piece_start = lax.axis_index("member") * section_rows
    anchors = regrouped.astype(jnp.float32)
    pull_sums = pull_total(anchors, regrouped, jnp.zeros_like(anchors))
    truth_rows = lax.dynamic_slice_in_dim(target, piece_start, section_rows, 1)
    weights = lax.dynamic_slice_in_dim(location_loss_factor, piece_start, section_rows, 0)
    patch_grad = score_grad(anchors, pull_sums, truth_rows, weights, ensemble)
    yielded_results = lax.all_to_all(
        patch_grad.reshape(ensemble, variable_total, 1, section_rows),
        "member",
        split_axis=0,
        concat_axis=2,
        tiled=True,
    )
    prediction_sensitivity = yielded_results.reshape(
        local_ensemble_slice, variable_total, location_entries
    )
    node_ids = jnp.arange(node_rows, dtype=jnp.int32)
    incidence = (local_assign[:, None] == node_ids[None, :]).astype(jnp.bfloat16)
    vertex_sensitivity = jnp.dot(
        prediction_sensitivity.reshape(local_ensemble_slice * variable_total, location_entries),
        incidence,
        preferred_element_type=jnp.float32,
    ).reshape(local_ensemble_slice, variable_total, node_rows)
    vertex_attribute_sensitivity = jnp.einsum(
        "mcn,cl->mnl",
        vertex_sensitivity,
        w_dec.astype(jnp.float32),
        precision=lax.Precision.HIGHEST,
    ).astype(jnp.bfloat16)
    return (prediction_sensitivity, vertex_attribute_sensitivity)


def solution(mesh):
    in_specs = (
        P("member", "node", None),
        P("member", None),
        P(None, "node"),
        P(),
        P(),
        P(),
        P(),
        P(),
        P("node"),
        P(None, "node"),
        P(None, "node"),
        P("node"),
    )
    out_specs = (P("member", None, "node"), P("member", "node", None))
    return jax.shard_map(
        per_device, mesh=mesh, in_specs=in_specs, out_specs=out_specs, check_vma=False
    )
```

profile of v0, /device:TPU:0, one launch (start us, length us, event | category | flops | bytes accessed | tf_op | source)
XLA Modules:
  0.0 91.4 jit_solution(5106094069198544770)
XLA Ops:
  0.7 1.3 %fusion = f32[2,256]{1,0:T(2,128)S(1)} fusion(bf16[2,256,512]{2,1,0:T(8,128)(2,1)} %param.16), kind=kLoop, calls=%fused_computation.25 | loop fusion | flops 785920 | bytes 526336 | tf_op jit(solution)/shard_map/reduce_sum | solution.py:30
  2.0 1.0 %convolution_add_fusion.2 = f32[2,512]{1,0:T(2,128)S(1)} fusion(f32[2,32]{1,0:T(2,128)} %param.17, f32[2,32,512]{2,1,0:T(8,128)} %param.19), kind=kOutput, calls=%fused_computation.24 | convolution fusion | flops 394240 | bytes 70656 | tf_op jit(solution)/shard_map/dot_general | solution.py:94
  3.0 1.2 %fusion.2 = bf16[2,256,512]{2,1,0:T(8,128)(2,1)S(1)} fusion(bf16[2,256,512]{2,1,0:T(8,128)(2,1)} %param.16, f32[2,512]{1,0:T(2,128)S(1)} %convolution_add_fusion.2, f32[2,256]{1,0:T(2,128)S(1)} %add_rsqrt_fusion.2), kind=kLoop, calls=%fused_computation.27 | loop fusion | flops 1048576 | bytes 1054720 | tf_op jit(solution)/shard_map/convert_element_type | solution.py:31
  4.3 0.5 collective-permute-start
  4.8 5.0 %collective-permute-start.1 = (bf16[2,96,512]{2,1,0:T(8,128)(2,1)S(1)}, bf16[2,96,512]{2,1,0:T(8,128)(2,1)S(1)}, u32[]{:S(2)}, u32[]{:S(2)}) collective-permute-start(bf16[2,96,512]{2,1,0:T(8,128)(2,1)S(1)} %get-tuple-element.68), channel_id=1, source_target_pairs={{1,0},{2,1},{3,2},{4,3},{5,4},{6,5},{7,6},{8,7},{9,8},{10,9},{11,1... | collective-permute-start | bytes 589832 | tf_op jit(solution)/shard_map/ppermute | solution.py:22
  10.1 0.3 reshape.94
  10.6 2.6 %collective-permute-done = bf16[2,96,512]{2,1,0:T(8,128)(2,1)S(1)} collective-permute-done((bf16[2,96,512]{2,1,0:T(8,128)(2,1)S(1)}, bf16[2,96,512]{2,1,0:T(8,128)(2,1)S(1)}, u32[]{:S(2)}, u32[]{:S(2)}) %collective-permute-start) | collective-permute-done | bytes 196640 | tf_op jit(solution)/shard_map/ppermute | solution.py:20
  13.3 0.9 %copy.133 = bf16[2,448,512]{2,0,1:T(2,128)(2,1)S(1)} copy(bf16[2,448,512]{2,1,0:T(8,128)(2,1)S(1)} %pad_maximum_fusion) | data formatting | bytes 1835008 | tf_op jit(solution)/shard_map/concatenate | solution.py:18
  14.3 1.7 %gather_fusion.1 = bf16[256,2,512]{2,1,0:T(2,128)(2,1)S(1)} fusion(bf16[2,448,512]{2,0,1:T(2,128)(2,1)S(1)} %copy.133, s32[1024]{0:T(1024)S(1)} %pad_clamp_fusion.5), kind=kCustom, calls=%fused_computation.clone | custom fusion | bytes 1049600 | tf_op jit(solution)/shard_map/jit(_take)/gather | solution.py:43
  16.0 1.7 %gather_fusion.2 = bf16[256,2,512]{2,1,0:T(2,128)(2,1)S(1)} fusion(bf16[2,448,512]{2,0,1:T(2,128)(2,1)S(1)} %copy.133, s32[1024]{0:T(1024)S(1)} %pad_clamp_fusion.4), kind=kCustom, calls=%fused_computation.1.clone | custom fusion | bytes 1049600 | tf_op jit(solution)/shard_map/jit(_take)/gather | solution.py:43
  17.8 1.7 %gather_fusion.3 = bf16[256,2,512]{2,1,0:T(2,128)(2,1)S(1)} fusion(bf16[2,448,512]{2,0,1:T(2,128)(2,1)S(1)} %copy.133, s32[1024]{0:T(1024)S(1)} %pad_clamp_fusion.3), kind=kCustom, calls=%fused_computation.2.clone | custom fusion | bytes 1049600 | tf_op jit(solution)/shard_map/jit(_take)/gather | solution.py:43
  19.5 2.5 %gather_fusion.4 = bf16[256,2,512]{2,1,0:T(2,128)(2,1)} fusion(bf16[2,448,512]{2,0,1:T(2,128)(2,1)S(1)} %copy.133, s32[1024]{0:T(1024)S(1)} %pad_clamp_fusion.2), kind=kCustom, calls=%fused_computation.3.clone | custom fusion | bytes 1049600 | tf_op jit(solution)/shard_map/jit(_take)/gather | solution.py:43
  22.0 2.5 %gather_fusion.5 = bf16[256,2,512]{2,1,0:T(2,128)(2,1)} fusion(bf16[2,448,512]{2,0,1:T(2,128)(2,1)S(1)} %copy.133, s32[1024]{0:T(1024)S(1)} %pad_clamp_fusion.1), kind=kCustom, calls=%fused_computation.4.clone | custom fusion | bytes 1049600 | tf_op jit(solution)/shard_map/jit(_take)/gather | solution.py:43
  24.5 2.5 %gather_fusion.6 = bf16[256,2,512]{2,1,0:T(2,128)(2,1)} fusion(bf16[2,448,512]{2,0,1:T(2,128)(2,1)S(1)} %copy.133, s32[1024]{0:T(1024)S(1)} %pad_clamp_fusion), kind=kCustom, calls=%fused_computation.5.clone | custom fusion | bytes 1049600 | tf_op jit(solution)/shard_map/jit(_take)/gather | solution.py:43
  27.0 2.8 %multiply_convert_fusion.5 = bf16[2,256,512]{2,1,0:T(8,128)(2,1)} fusion(bf16[256,2,512]{2,1,0:T(2,128)(2,1)} %gather_fusion.6, bf16[256,2,512]{2,1,0:T(2,128)(2,1)} %gather_fusion.5, bf16[256,2,512]{2,1,0:T(2,128)(2,1)} %gather_fusion.4, bf16[256,2,512]{2,1,0:T(2,128)(2,1)S(1)} %gather_fusion.3, bf16[256,2,512]{2,1,0:T(2,128)(2,1)S(1)} %gather_fusion.2, ...), kind=kLoop, calls=%fused_computation.48 | loop fusion | flops 4980736 | bytes 3671552 | tf_op jit(solution)/shard_map/convert_element_type | solution.py:46
  29.8 2.7 %multiply_reduce_fusion.2 = (f32[2,256]{1,0:T(2,128)S(1)}, f32[2,256,512]{2,1,0:T(8,128)S(1)}) fusion(bf16[2,512,512]{2,1,0:T(8,128)(2,1)} %param.21, bf16[2,1024,512]{2,1,0:T(8,128)(2,1)} %param.20, bf16[2,256,512]{2,1,0:T(8,128)(2,1)} %multiply_convert_fusion.5, bf16[2,256,512]{2,1,0:T(8,128)(2,1)S(1)} %fusion.2, bf16[2,256,512]{2,1,0:T(8,128)(2,1)S(1)} %copy-done.1), kind=kOutput, calls=%fused_computation.45 | convolution fusion | flops 809762304 | bytes 4196352 | tf_op jit(solution)/shard_map/mrk,kl->mrl/dot_general | solution.py:53
  32.6 0.2 multiply_convert_fusion.3
  32.8 1.4 %collective-permute-start.2 = (bf16[2,96,512]{2,1,0:T(8,128)(2,1)S(1)}, bf16[2,96,512]{2,1,0:T(8,128)(2,1)S(1)}, u32[]{:S(2)}, u32[]{:S(2)}) collective-permute-start(bf16[2,96,512]{2,1,0:T(8,128)(2,1)S(1)} %get-tuple-element.65), channel_id=1, source_target_pairs={{0,1},{1,2},{2,3},{3,4},{4,5},{5,6},{6,7},{7,8},{8,9},{9,10},{10,1... | collective-permute-start | bytes 589832 | tf_op jit(solution)/shard_map/ppermute | solution.py:20
  34.2 3.3 %collective-permute-start.3 = (bf16[2,96,512]{2,1,0:T(8,128)(2,1)S(1)}, bf16[2,96,512]{2,1,0:T(8,128)(2,1)S(1)}, u32[]{:S(2)}, u32[]{:S(2)}) collective-permute-start(bf16[2,96,512]{2,1,0:T(8,128)(2,1)S(1)} %get-tuple-element.66), channel_id=1, source_target_pairs={{1,0},{2,1},{3,2},{4,3},{5,4},{6,5},{7,6},{8,7},{9,8},{10,9},{11,1... | collective-permute-start | bytes 589832 | tf_op jit(solution)/shard_map/ppermute | solution.py:22
  37.5 3.2 %collective-permute-done.2 = bf16[2,96,512]{2,1,0:T(8,128)(2,1)S(1)} collective-permute-done((bf16[2,96,512]{2,1,0:T(8,128)(2,1)S(1)}, bf16[2,96,512]{2,1,0:T(8,128)(2,1)S(1)}, u32[]{:S(2)}, u32[]{:S(2)}) %collective-permute-start.2) | collective-permute-done | bytes 196640 | tf_op jit(solution)/shard_map/ppermute | solution.py:20
  40.8 0.9 %copy.145 = bf16[2,448,512]{2,0,1:T(2,128)(2,1)S(1)} copy(bf16[2,448,512]{2,1,0:T(8,128)(2,1)S(1)} %pad_maximum_fusion.1) | data formatting | bytes 1835008 | tf_op jit(solution)/shard_map/concatenate | solution.py:18
  41.7 1.7 %gather_fusion.7 = bf16[256,2,512]{2,1,0:T(2,128)(2,1)S(1)} fusion(bf16[2,448,512]{2,0,1:T(2,128)(2,1)S(1)} %copy.145, s32[1024]{0:T(1024)S(1)} %pad_clamp_fusion.5), kind=kCustom, calls=%fused_computation.6.clone | custom fusion | bytes 1049600 | tf_op jit(solution)/shard_map/jit(_take)/gather | solution.py:43
  43.5 1.7 %gather_fusion.8 = bf16[256,2,512]{2,1,0:T(2,128)(2,1)S(1)} fusion(bf16[2,448,512]{2,0,1:T(2,128)(2,1)S(1)} %copy.145, s32[1024]{0:T(1024)S(1)} %pad_clamp_fusion.4), kind=kCustom, calls=%fused_computation.7.clone | custom fusion | bytes 1049600 | tf_op jit(solution)/shard_map/jit(_take)/gather | solution.py:43
  45.2 1.7 %gather_fusion.9 = bf16[256,2,512]{2,1,0:T(2,128)(2,1)S(1)} fusion(bf16[2,448,512]{2,0,1:T(2,128)(2,1)S(1)} %copy.145, s32[1024]{0:T(1024)S(1)} %pad_clamp_fusion.3), kind=kCustom, calls=%fused_computation.8.clone | custom fusion | bytes 1049600 | tf_op jit(solution)/shard_map/jit(_take)/gather | solution.py:43
  47.0 2.5 %gather_fusion.10 = bf16[256,2,512]{2,1,0:T(2,128)(2,1)} fusion(bf16[2,448,512]{2,0,1:T(2,128)(2,1)S(1)} %copy.145, s32[1024]{0:T(1024)S(1)} %pad_clamp_fusion.2), kind=kCustom, calls=%fused_computation.9.clone | custom fusion | bytes 1049600 | tf_op jit(solution)/shard_map/jit(_take)/gather | solution.py:43
  49.5 2.5 %gather_fusion.11 = bf16[256,2,512]{2,1,0:T(2,128)(2,1)} fusion(bf16[2,448,512]{2,0,1:T(2,128)(2,1)S(1)} %copy.145, s32[1024]{0:T(1024)S(1)} %pad_clamp_fusion.1), kind=kCustom, calls=%fused_computation.10.clone | custom fusion | bytes 1049600 | tf_op jit(solution)/shard_map/jit(_take)/gather | solution.py:43
  52.0 2.5 %gather_fusion.12 = bf16[256,2,512]{2,1,0:T(2,128)(2,1)} fusion(bf16[2,448,512]{2,0,1:T(2,128)(2,1)S(1)} %copy.145, s32[1024]{0:T(1024)S(1)} %pad_clamp_fusion), kind=kCustom, calls=%fused_computation.11.clone | custom fusion | bytes 1049600 | tf_op jit(solution)/shard_map/jit(_take)/gather | solution.py:43
  54.5 2.7 %multiply_convert_fusion.2 = bf16[2,256,512]{2,1,0:T(8,128)(2,1)} fusion(bf16[256,2,512]{2,1,0:T(2,128)(2,1)} %gather_fusion.12, bf16[256,2,512]{2,1,0:T(2,128)(2,1)} %gather_fusion.11, bf16[256,2,512]{2,1,0:T(2,128)(2,1)} %gather_fusion.10, bf16[256,2,512]{2,1,0:T(2,128)(2,1)S(1)} %gather_fusion.9, bf16[256,2,512]{2,1,0:T(2,128)(2,1)S(1)} %gather_fusion.8, ...), kind=kLoop, calls=%fused_computation.43 | loop fusion | flops 4980736 | bytes 3671552 | tf_op jit(solution)/shard_map/convert_element_type | solution.py:46
  57.2 3.1 %multiply_reduce_fusion.1 = (f32[2,256]{1,0:T(2,128)S(1)}, f32[2,256,512]{2,1,0:T(8,128)S(1)}) fusion(f32[2,256,512]{2,1,0:T(8,128)} %copy-done.2, bf16[2,512,512]{2,1,0:T(8,128)(2,1)} %param.21, bf16[2,1024,512]{2,1,0:T(8,128)(2,1)} %param.20, bf16[2,256,512]{2,1,0:T(8,128)(2,1)} %multiply_convert_fusion.2, bf16[2,256,512]{2,1,0:T(8,128)(2,1)S(1)} %multiply_convert_fusion.3), kind=kOutput, calls=%fused_computation.40 | convolution fusion | flops 809500160 | bytes 4720640 | tf_op jit(solution)/shard_map/mrk,kl->mrl/dot_general | solution.py:53
  60.3 0.4 convolution_bitcast_fusion
  60.7 0.2 copy.157
  60.9 3.6 %gather_fusion = f32[1024,2,83]{2,1,0:T(2,128)S(1)} fusion(f32[2,83,256]{1,0,2:T(2,128)S(1)} %copy.157, s32[1024]{0:T(1024)S(1)} %fusion.53), kind=kCustom, calls=%fused_computation.12 | custom fusion | bytes 1363968 | tf_op jit(solution)/shard_map/jit(_take)/gather | solution.py:115
  64.5 0.8 copy.166
  65.2 0.4 add_convert_fusion
  65.6 1.0 %copy.159 = bf16[2,83,2,512]{3,0,1,2:T(2,128)(2,1)} copy(bf16[2,83,2,512]{3,2,0,1:T(2,128)(2,1)S(1)} %add_convert_fusion) | data formatting | bytes 679936 | tf_op jit(solution)/shard_map/convert_element_type | solution.py:116
  66.6 3.7 %all-to-all-start = ((bf16[2,83,2,512]{3,0,1,2:T(2,128)(2,1)}), bf16[2,83,2,512]{3,0,1,2:T(2,128)(2,1)S(1)}, u32[]{:S(2)}, u32[]{:S(2)}) async-start(bf16[2,83,2,512]{3,0,1,2:T(2,128)(2,1)} %copy.159), calls=%async_computation | async-start | bytes 679936 | tf_op jit(solution)/shard_map/all_to_all | solution.py:125
  70.4 7.0 %all-to-all-done = bf16[2,83,2,512]{3,0,1,2:T(2,128)(2,1)S(1)} async-done(((bf16[2,83,2,512]{3,0,1,2:T(2,128)(2,1)}), bf16[2,83,2,512]{3,0,1,2:T(2,128)(2,1)S(1)}, u32[]{:S(2)}, u32[]{:S(2)}) %all-to-all-start) | async-done | bytes 340000 | tf_op jit(solution)/shard_map/all_to_all | solution.py:125
  77.6 1.9 %while.11 = (s32[]{:T(128)}, f32[4,83,512]{2,1,0:T(8,128)S(1)}, bf16[4,83,512]{2,1,0:T(8,128)(2,1)S(1)}, f32[4,83,512]{2,1,0:T(8,128)S(1)}, s32[]{:T(128)}, /*index=5*/s32[]{:T(128)}) while((s32[]{:T(128)}, f32[4,83,512]{2,1,0:T(8,128)S(1)}, bf16[4,83,512]{2,1,0:T(8,128)(2,1)S(1)}, f32[4,83,512]{2,1,0:T(8,128)S(1)}, s32[]{:T(128)}, ...), condition=%wide.region_6.8_spmd.clone, body=%wide.region_4.7_spmd.clone.sunk | while | flops 1232387 | bytes 3347539 | solution.py:63
  77.8 0.3 select_add_fusion.2
  78.3 0.3 select_add_fusion.2
  78.7 0.3 select_add_fusion.2
  79.2 0.3 select_add_fusion.2
  79.7 0.2 fusion.44
  79.9 9.0 %all_to_all.30 = bf16[4,83,1,512]{3,1,2,0:T(8,128)(2,1)S(1)} all-to-all(bf16[4,83,1,512]{3,1,2,0:T(8,128)(2,1)S(1)} %fusion.44), channel_id=1, replica_groups=mesh['member'=2,'node'=16] {'member'}, dimensions={0} | all-to-all | bytes 679936 | tf_op jit(solution)/shard_map/all_to_all | solution.py:134
  88.9 0.4 copy.213
  89.3 0.2 reshape.92
  89.5 0.4 fusion.16
  89.9 1.4 %convolution_convert_fusion = bf16[2,256,512]{2,1,0:T(8,128)(2,1)} fusion(f32[2,83,256]{2,1,0:T(8,128)S(1)} %fusion.16, bf16[83,512]{1,0:T(8,128)(2,1)S(1)} %copy-done), kind=kOutput, calls=%fused_computation.21 | convolution fusion | flops 261357568 | bytes 779264 | tf_op jit(solution)/shard_map/mcn,cl->mnl/dot_general | solution.py:151
  (68 shorter events, 1.5 us)
Async XLA Ops:
  0.6 59.7 %copy-start = (bf16[83,512]{1,0:T(8,128)(2,1)S(1)}, bf16[83,512]{1,0:T(8,128)(2,1)}, u32[]{:S(2)}) copy-start(bf16[83,512]{1,0:T(8,128)(2,1)} %param.23) | copy-start | bytes 254980
  0.6 9.8 %copy-start.8 = (f32[2,32]{1,0:T(2,128)S(1)}, f32[2,32]{1,0:T(2,128)}, u32[]{:S(2)}) copy-start(f32[2,32]{1,0:T(2,128)} %param.17) | copy-start | bytes 772
  0.7 9.8 %copy-start.5 = (f32[2,32,512]{2,1,0:T(8,128)S(1)}, f32[2,32,512]{2,1,0:T(8,128)}, u32[]{:S(2)}) copy-start(f32[2,32,512]{2,1,0:T(8,128)} %param.19) | copy-start | bytes 393220
  0.7 9.2 %copy-start.7 = (s32[6,256]{1,0:T(8,128)S(1)}, s32[6,256]{1,0:T(8,128)}, u32[]{:S(2)}) copy-start(s32[6,256]{1,0:T(8,128)} %param.18) | copy-start | bytes 18436
  0.7 9.4 %copy-start.9 = (s32[1024]{0:T(1024)S(1)}, s32[1024]{0:T(1024)}, u32[]{:S(2)}) copy-start(s32[1024]{0:T(1024)} %param.24) | copy-start | bytes 12292
  0.7 9.4 %copy-start.4 = (bf16[83,1024]{1,0:T(8,128)(2,1)S(1)}, bf16[83,1024]{1,0:T(8,128)(2,1)}, u32[]{:S(2)}) copy-start(bf16[83,1024]{1,0:T(8,128)(2,1)} %param.25) | copy-start | bytes 509956
  4.3 9.0 %collective-permute-start = (bf16[2,96,512]{2,1,0:T(8,128)(2,1)S(1)}, bf16[2,96,512]{2,1,0:T(8,128)(2,1)S(1)}, u32[]{:S(2)}, u32[]{:S(2)}) collective-permute-start(bf16[2,96,512]{2,1,0:T(8,128)(2,1)S(1)} %get-tuple-element.67), channel_id=1, source_target_pairs={{0,1},{1,2},{2,3},{3,4},{4,5},{5,6},{6,7},{7,8},{8,9},{9,10},{10,1... | collective-permute-start | bytes 589832 | tf_op jit(solution)/shard_map/ppermute | solution.py:20
  4.8 8.4 %collective-permute-start.1 = (bf16[2,96,512]{2,1,0:T(8,128)(2,1)S(1)}, bf16[2,96,512]{2,1,0:T(8,128)(2,1)S(1)}, u32[]{:S(2)}, u32[]{:S(2)}) collective-permute-start(bf16[2,96,512]{2,1,0:T(8,128)(2,1)S(1)} %get-tuple-element.68), channel_id=1, source_target_pairs={{1,0},{2,1},{3,2},{4,3},{5,4},{6,5},{7,6},{8,7},{9,8},{10,9},{11,1... | collective-permute-start | bytes 589832 | tf_op jit(solution)/shard_map/ppermute | solution.py:22
  27.0 2.8 %copy-start.1 = (bf16[2,256,512]{2,1,0:T(8,128)(2,1)S(1)}, bf16[2,256,512]{2,1,0:T(8,128)(2,1)}, u32[]{:S(2)}) copy-start(bf16[2,256,512]{2,1,0:T(8,128)(2,1)} %param.16) | copy-start | bytes 1572868
  32.5 8.2 %copy-start.2 = (f32[2,256,512]{2,1,0:T(8,128)}, f32[2,256,512]{2,1,0:T(8,128)S(1)}, u32[]{:S(2)}) copy-start(f32[2,256,512]{2,1,0:T(8,128)S(1)} %get-tuple-element.76) | copy-start | bytes 3145732
  32.8 7.9 %collective-permute-start.2 = (bf16[2,96,512]{2,1,0:T(8,128)(2,1)S(1)}, bf16[2,96,512]{2,1,0:T(8,128)(2,1)S(1)}, u32[]{:S(2)}, u32[]{:S(2)}) collective-permute-start(bf16[2,96,512]{2,1,0:T(8,128)(2,1)S(1)} %get-tuple-element.65), channel_id=1, source_target_pairs={{0,1},{1,2},{2,3},{3,4},{4,5},{5,6},{6,7},{7,8},{8,9},{9,10},{10,1... | collective-permute-start | bytes 589832 | tf_op jit(solution)/shard_map/ppermute | solution.py:20
  34.2 6.5 %collective-permute-start.3 = (bf16[2,96,512]{2,1,0:T(8,128)(2,1)S(1)}, bf16[2,96,512]{2,1,0:T(8,128)(2,1)S(1)}, u32[]{:S(2)}, u32[]{:S(2)}) collective-permute-start(bf16[2,96,512]{2,1,0:T(8,128)(2,1)S(1)} %get-tuple-element.66), channel_id=1, source_target_pairs={{1,0},{2,1},{3,2},{4,3},{5,4},{6,5},{7,6},{8,7},{9,8},{10,9},{11,1... | collective-permute-start | bytes 589832 | tf_op jit(solution)/shard_map/ppermute | solution.py:22
  57.2 3.1 %copy-start.10 = (f32[512]{0:T(512)S(1)}, f32[512]{0:T(512)}, u32[]{:S(2)}) copy-start(f32[512]{0:T(512)} %param.22) | copy-start | bytes 6148
  64.4 5.9 %copy-start.11 = (f32[1024]{0:T(1024)S(1)}, f32[1024]{0:T(1024)}, u32[]{:S(2)}) copy-start(f32[1024]{0:T(1024)} %param.27) | copy-start | bytes 12292
  64.4 6.0 %copy-start.6 = (bf16[83,1024]{1,0:T(8,128)(2,1)S(1)}, bf16[83,1024]{1,0:T(8,128)(2,1)}, u32[]{:S(2)}) copy-start(bf16[83,1024]{1,0:T(8,128)(2,1)} %param.26) | copy-start | bytes 509956
  66.6 10.8 %all-to-all-start = ((bf16[2,83,2,512]{3,0,1,2:T(2,128)(2,1)}), bf16[2,83,2,512]{3,0,1,2:T(2,128)(2,1)S(1)}, u32[]{:S(2)}, u32[]{:S(2)}) async-start(bf16[2,83,2,512]{3,0,1,2:T(2,128)(2,1)} %copy.159), calls=%async_computation | async-start | bytes 679936 | tf_op jit(solution)/shard_map/all_to_all | solution.py:125
  89.5 1.9 %copy-start.3 = (bf16[2,83,1024]{2,0,1:T(2,128)(2,1)}, bf16[2,83,1024]{2,0,1:T(2,128)(2,1)S(1)}, u32[]{:S(2)}) copy-start(bf16[2,83,1024]{2,0,1:T(2,128)(2,1)S(1)} %reshape.92) | copy-start | bytes 1019908
where the time goes:
time: 91.8 us; the launch traced here: 91.4 us
  local copies, waits for them, and re-layouts  34 us (37%)
  starting transfers between devices  14 us (15%)
  waiting for transfers between devices  12.9 us (14%)
  other arithmetic  11 us (12%)
  matrix products  9.18 us (10%)
  blocking collectives  8.99 us (10%)
  between operations  1.09 us (1%)
    gather x12, local copies, waits for them, and re-layouts, neighbour_mean(): jnp.take(normalized_rows, margin + positions + offsets, axis=1)  25.5 us
    all_to_all x1, blocking collectives, per_device(): lax.all_to_all(patch_grad.reshape(ensemble, variable_total, 1, section_ro...  8.99 us
    ppermute x2, starting transfers between devices, extended(): lax.ppermute(head, axis, [((i + 1) % count, i) for i in range(count)])  8.31 us
    all_to_all x1, waiting for transfers between devices, per_device(): lax.all_to_all(partition_pieces, 'member', split_axis=2, concat_axis=0, t...  7.01 us
    ppermute x2, waiting for transfers between devices, extended(): lax.ppermute(tail, axis, [(i, (i + 1) % count) for i in range(count)])  5.88 us
    dot_general x2, matrix products, layer_update(): jnp.einsum('mrk,kl->mrl', activated, w_out_layer, preferred_element_type=...  5.79 us
    convert_element_type x2, other arithmetic, neighbour_mean(): return (summed / mesh_links.shape[0]).astype(jnp.bfloat16)  5.52 us
    gather x2, local copies, waits for them, and re-layouts, per_device(): jnp.take(readout_result, local_assign, axis=2)  4.31 us
  transfers between devices with their start and end apart: 5, of which 3 were waited for; matrix products, arithmetic and copies ran while one was open for 1% of the time, Pallas kernels for 0%

commit v1 on v0

v1 whole, which is shorter than its diff:
```python
import functools

import jax
import jax.numpy as jnp
from jax import lax
from jax.experimental import pallas as pl
from jax.experimental.pallas import tpu as pltpu
from jax.sharding import PartitionSpec as P

WIN = 96
NORM_EPS = 1e-06
DIST_EPS = 1e-06
PLANES = 2
LANES = 128
F32 = jnp.float32
BF16 = jnp.bfloat16

NT = (((1,), (1,)), ((), ()))


def dot(a, b):
    return jnp.dot(a, b, preferred_element_type=F32)


def norm(values, gain):
    inverse = lax.rsqrt(jnp.mean(values * values, axis=-1, keepdims=True) + NORM_EPS)
    return (values * inverse * gain).astype(BF16)


def kernel(
    groups,
    shards,
    latent,
    noise,
    links,
    w_cond,
    dec_gain,
    w_dec,
    vertex_map,
    weights,
    w_in,
    w_out,
    prior_hbm,
    target_hbm,
    sens,
    vas,
    wi,
    wo,
    prior,
    target,
    state,
    normed,
    halo,
    part,
    pre,
    count_own,
    count_halo,
    onehot,
    wdp,
    dec,
    dec_in,
    own,
    other,
    load_sem,
    hs_sem,
    hr_sem,
    ds_sem,
    dr_sem,
):
    members, rows, width = latent.shape
    layers = w_in.shape[0]
    slots = links.shape[0]
    channels = w_dec.shape[0]
    points = vertex_map.shape[1]
    padded = wdp.shape[0]
    me = lax.axis_index("node")
    mine = lax.axis_index("member")
    right = lax.rem(me + 1, shards)
    left = lax.rem(me + shards - 1, shards)
    peers = [lax.rem(mine + k, groups) for k in range(1, groups)]

    barrier = pltpu.get_barrier_semaphore()
    for node in (left, right):
        pl.semaphore_signal(barrier, inc=1, device_id={"node": node}, device_id_type=pl.DeviceIdType.MESH)
    for peer in peers:
        pl.semaphore_signal(barrier, inc=1, device_id={"member": peer}, device_id_type=pl.DeviceIdType.MESH)

    loads = []
    for l in range(layers):
        loads.append(pltpu.make_async_copy(w_in.at[l], wi.at[l], load_sem.at[2 * l]))
        loads.append(pltpu.make_async_copy(w_out.at[l], wo.at[l], load_sem.at[2 * l + 1]))
    loads.append(pltpu.make_async_copy(prior_hbm, prior, load_sem.at[2 * layers]))
    loads.append(pltpu.make_async_copy(target_hbm, target, load_sem.at[2 * layers + 1]))
    for load in loads:
        load.start()

    gains = [
        1.0
        + jnp.dot(
            noise[...],
            w_cond[l],
            precision=lax.Precision.HIGHEST,
            preferred_element_type=F32,
        )
        for l in range(layers)
    ]

    halo_copies = {}

    def send_halo(l, m):
        pair = [
            pltpu.make_async_remote_copy(
                src_ref=normed.at[l, m, pl.ds(rows - WIN, WIN)],
                dst_ref=halo.at[l, m, pl.ds(0, WIN)],
                send_sem=hs_sem.at[l, m, 0],
                recv_sem=hr_sem.at[l, m, 0],
                device_id={"node": right},
                device_id_type=pl.DeviceIdType.MESH,
            ),
            pltpu.make_async_remote_copy(
                src_ref=normed.at[l, m, pl.ds(0, WIN)],
                dst_ref=halo.at[l, m, pl.ds(WIN, WIN)],
                send_sem=hs_sem.at[l, m, 1],
                recv_sem=hr_sem.at[l, m, 1],
                device_id={"node": left},
                device_id_type=pl.DeviceIdType.MESH,
            ),
        ]
        for copy in pair:
            copy.start()
        halo_copies[l, m] = pair

    for m in range(members):
        values = latent[m].astype(F32)
        normed[0, m] = norm(values, gains[0][m : m + 1])
        state[m] = values
        if m == 0:
            pl.semaphore_wait(barrier, 2 + len(peers))
        send_halo(0, m)

    total = rows * shards
    place = lax.rem(links[...] - (me * rows - WIN) + total, total)
    ids = lax.broadcasted_iota(jnp.int32, (rows, rows), 0) + WIN
    counts = jnp.zeros((rows, rows), F32)
    for k in range(slots):
        counts = counts + jnp.where(ids == place[k : k + 1, :], 1.0, 0.0)
    count_own[...] = counts.T.astype(BF16)
    ids = lax.broadcasted_iota(jnp.int32, (2 * WIN, rows), 0)
    ids = jnp.where(ids < WIN, ids, ids + rows)
    counts = jnp.zeros((2 * WIN, rows), F32)
    for k in range(slots):
        counts = counts + jnp.where(ids == place[k : k + 1, :], 1.0, 0.0)
    count_halo[...] = counts.T.astype(BF16)

    def own_part(l, m):
        rows_bf = normed[l, m]
        part[m] = dot(count_own[...], rows_bf)
        pre[m] = dot(rows_bf, wi[l, 0:width])

    dec_copies = []
    for l in range(layers):
        loads[2 * l].wait()
        for m in range(members):
            own_part(l, m)
        if l == 0:
            local = vertex_map[...] - me * rows
            nodes = lax.broadcasted_iota(jnp.int32, (rows, points), 0)
            onehot[...] = jnp.where(nodes == local, 1.0, 0.0).astype(BF16)
            wdp[...] = jnp.zeros_like(wdp)
            wdp[0:channels] = w_dec[...]
        loads[2 * l + 1].wait()
        for m in range(members):
            for copy in halo_copies[l, m]:
                copy.wait_recv()
            summed = part[m] + dot(count_halo[...], halo[l, m])
            neighbours = (summed * (1.0 / slots)).astype(BF16)
            preact = pre[m] + dot(neighbours, wi[l, width : 2 * width])
            activated = (preact / (1.0 + jnp.exp(-preact))).astype(BF16)
            values = state[m] + dot(activated, wo[l])
            if l + 1 < layers:
                state[m] = values
                normed[l + 1, m] = norm(values, gains[l + 1][m : m + 1])
                send_halo(l + 1, m)
            else:
                features = norm(values, dec_gain[...])
                decoded = lax.dot_general(wdp[...], features, NT, preferred_element_type=F32)
                for plane in range(PLANES):
                    piece = decoded.astype(BF16)
                    dec[m, plane] = piece
                    if plane + 1 < PLANES:
                        decoded = decoded - piece.astype(F32)
                for k, peer in enumerate(peers):
                    copy = pltpu.make_async_remote_copy(
                        src_ref=dec.at[m],
                        dst_ref=dec_in.at[k, m],
                        send_sem=ds_sem.at[k, m],
                        recv_sem=dr_sem.at[k, m],
                        device_id={"member": peer},
                        device_id_type=pl.DeviceIdType.MESH,
                    )
                    copy.start()
                    dec_copies.append((k, m, copy))

    for load in loads[2 * layers :]:
        load.wait()

    def forecast(planes):
        gathered = dot(planes[0], onehot[...])
        for plane in range(1, PLANES):
            gathered = gathered + dot(planes[plane], onehot[...])
        return (gathered[0:channels] + prior[...].astype(F32)).astype(BF16)

    for m in range(members):
        own[m] = forecast([dec[m, plane] for plane in range(PLANES)])
    for k, m, copy in dec_copies:
        copy.wait_recv()
        other[k * members + m] = forecast([dec_in[k, m, plane] for plane in range(PLANES)])

    ensemble = members * groups

    def unit(offset):
        return offset * lax.rsqrt(jnp.sum(offset * offset, axis=0, keepdims=True) + DIST_EPS)

    def points_step(step, carry):
        cut = pl.ds(pl.multiple_of(step * LANES, LANES), LANES)
        anchors = [own[m, :, cut].astype(F32) for m in range(members)]
        pulls = [None] * members

        def add(m, value):
            pulls[m] = value if pulls[m] is None else pulls[m] + value

        for a in range(members):
            for b in range(a + 1, members):
                pull = unit(anchors[a] - anchors[b])
                add(a, pull)
                add(b, -pull)
        for b in range(other.shape[0]):
            values = other[b, :, cut].astype(F32)
            for a in range(members):
                add(a, unit(anchors[a] - values))
        truth = target[:, cut].astype(F32)
        weight = weights[:, cut]
        for a in range(members):
            skill = unit(anchors[a] - truth) * (1.0 / ensemble)
            if ensemble > 1:
                skill = skill - pulls[a] * (1.0 / (ensemble * (ensemble - 1)))
            sens[a, :, cut] = (weight * skill).astype(BF16)
        return carry

    lax.fori_loop(0, points // LANES, points_step, 0)

    for m in range(members):
        node_grad = lax.dot_general(onehot[...], sens[m], NT, preferred_element_type=F32)
        high = node_grad.astype(BF16)
        low = (node_grad - high.astype(F32)).astype(BF16)
        vas[m] = (dot(high, w_dec[...]) + dot(low, w_dec[...])).astype(BF16)

    for pair in halo_copies.values():
        for copy in pair:
            copy.wait_send()
    for _, _, copy in dec_copies:
        copy.wait_send()


def per_device(
    latent,
    noise_draw,
    mesh_links,
    w_cond,
    w_in,
    w_out,
    dec_gain,
    w_dec,
    target_vertex_map,
    prior_field,
    target,
    location_loss_factor,
):
    groups = lax.axis_size("member")
    shards = lax.axis_size("node")
    members, rows, width = latent.shape
    layers = w_in.shape[0]
    channels = w_dec.shape[0]
    points = target_vertex_map.shape[0]
    padded = -(-channels // 16) * 16
    vmem = pl.BlockSpec(memory_space=pltpu.VMEM)
    hbm = pl.BlockSpec(memory_space=pl.ANY)
    far = max(groups - 1, 1)
    return pl.pallas_call(
        functools.partial(kernel, groups, shards),
        out_shape=(
            jax.ShapeDtypeStruct((members, channels, points), BF16),
            jax.ShapeDtypeStruct((members, rows, width), BF16),
        ),
        in_specs=[vmem] * 8 + [hbm] * 4,
        out_specs=(vmem, vmem),
        scratch_shapes=[
            pltpu.VMEM(w_in.shape, BF16),
            pltpu.VMEM(w_out.shape, BF16),
            pltpu.VMEM((channels, points), BF16),
            pltpu.VMEM((channels, points), BF16),
            pltpu.VMEM((members, rows, width), F32),
            pltpu.VMEM((layers, members, rows, width), BF16),
            pltpu.VMEM((layers, members, 2 * WIN, width), BF16),
            pltpu.VMEM((members, rows, width), F32),
            pltpu.VMEM((members, rows, width), F32),
            pltpu.VMEM((rows, rows), BF16),
            pltpu.VMEM((rows, 2 * WIN), BF16),
            pltpu.VMEM((rows, points), BF16),
            pltpu.VMEM((padded, width), BF16),
            pltpu.VMEM((members, PLANES, padded, rows), BF16),
            pltpu.VMEM((far, members, PLANES, padded, rows), BF16),
            pltpu.VMEM((members, channels, points), BF16),
            pltpu.VMEM((far * members, channels, points), BF16),
            pltpu.SemaphoreType.DMA((2 * layers + 2,)),
            pltpu.SemaphoreType.DMA((layers, members, 2)),
            pltpu.SemaphoreType.DMA((layers, members, 2)),
            pltpu.SemaphoreType.DMA((far, members)),
            pltpu.SemaphoreType.DMA((far, members)),
        ],
        compiler_params=pltpu.CompilerParams(
            collective_id=0, has_side_effects=True, vmem_limit_bytes=62 * 1024 * 1024
        ),
    )(
        latent,
        noise_draw,
        mesh_links,
        w_cond,
        dec_gain.reshape(1, width),
        w_dec,
        target_vertex_map.reshape(1, points),
        location_loss_factor.reshape(1, points),
        w_in,
        w_out,
        prior_field,
        target,
    )


def solution(mesh):
    in_specs = (
        P("member", "node", None),
        P("member", None),
        P(None, "node"),
        P(),
        P(),
        P(),
        P(),
        P(),
        P("node"),
        P(None, "node"),
        P(None, "node"),
        P("node"),
    )
    out_specs = (P("member", None, "node"), P("member", "node", None))
    return jax.shard_map(
        per_device, mesh=mesh, in_specs=in_specs, out_specs=out_specs, check_vma=False
    )
```

time: 91.8 us -> 30.8 us (0.34)
  local copies, waits for them, and re-layouts: 34 us -> 3.93 us
  Pallas kernels: 0 us -> 26 us
  starting transfers between devices: 14 us -> 0 us
  waiting for transfers between devices: 12.9 us -> 0 us
  other arithmetic: 11 us -> 0 us
  matrix products: 9.18 us -> 0 us
  blocking collectives: 8.99 us -> 0 us
    gather x14 -> x0, local copies, waits for them, and re-layouts: 29.8 us -> none  [the longest x12 25.5 us: neighbour_mean(): jnp.take(normalized_rows, margin + positions + offsets, axis=1)]
    pallas_call x0 -> x1, Pallas kernels: none -> 26 us  [per_device(): pl.pallas_call(functools.partial(kernel, groups, shards), out_shape=(jax....]
    ppermute x4 -> x0, starting transfers between devices: 10.3 us -> none  [the longest x2 8.31 us: extended(): lax.ppermute(head, axis, [((i + 1) % count, i) for i in range(count)])]
    dot_general x7 -> x0, matrix products: 9.18 us -> none  [the longest x2 5.79 us: layer_update(): jnp.einsum('mrk,kl->mrl', activated, w_out_layer, preferred_element_type=...]
    all_to_all x1 -> x0, blocking collectives: 8.99 us -> none  [per_device(): lax.all_to_all(patch_grad.reshape(ensemble, variable_total, 1, section_ro...]
    convert_element_type x7 -> x0, other arithmetic: 7.43 us -> none  [the longest x2 5.52 us: neighbour_mean(): return (summed / mesh_links.shape[0]).astype(jnp.bfloat16)]
    all_to_all x1 -> x0, waiting for transfers between devices: 7.01 us -> none  [per_device(): lax.all_to_all(partition_pieces, 'member', split_axis=2, concat_axis=0, t...]
    ppermute x4 -> x0, waiting for transfers between devices: 5.88 us -> none  [the longest x2 5.88 us: extended(): lax.ppermute(tail, axis, [(i, (i + 1) % count) for i in range(count)])]
  transfers between devices with their start and end apart: 5 -> 0, of which waited for: 3 -> 0; matrix products, arithmetic and copies ran while one was open for 1% -> 0% of each run, Pallas kernels for 0% -> 0%
where the time goes in v1:
time: 30.8 us; the launch traced here: 30.5 us
  Pallas kernels  26 us (84%)
  local copies, waits for them, and re-layouts  3.93 us (13%)
  between operations  0.64 us (2%)
    pallas_call x1, Pallas kernels, per_device(): pl.pallas_call(functools.partial(kernel, groups, shards), out_shape=(jax....  26 us
    pallas_call x1, local copies, waits for them, and re-layouts, per_device(): pl.pallas_call(functools.partial(kernel, groups, shards), out_shape=(jax....  2.06 us
    unnamed x1, local copies, waits for them, and re-layouts  1.87 us

profile of v1, /device:TPU:0, one launch (start us, length us, event | category | flops | bytes accessed | tf_op | source)
XLA Modules:
  0.0 30.5 jit_solution(8473035680652662977)
XLA Ops:
  0.6 26.0 %shard_map.131 = (bf16[2,83,1024]{2,1,0:T(8,128)(2,1)}, bf16[2,256,512]{2,1,0:T(8,128)(2,1)}) custom-call(bf16[2,256,512]{2,1,0:T(8,128)(2,1)} %latent.1, f32[2,32]{1,0:T(2,128)} %noise.1, s32[6,256]{1,0:T(8,128)} %links.1, f32[2,32,512]{2,1,0:T(8,128)} %w_cond.1, f32[1,512]{1,0:T(1,128)} %bitcast.5, bf16[83,512]{1,0:T(8,128)(2,1)} %w_dec.1, ...), custom_call_target="tpu_custom_call" | custom-call | tf_op jit(solution)/shard_map/pallas_call | solution.py:289
  26.6 2.1 %copy.14 = bf16[2,83,1024]{2,0,1:T(2,128)(2,1)} copy(bf16[2,83,1024]{2,1,0:T(8,128)(2,1)} %get-tuple-element.2) | data formatting | bytes 679936 | tf_op jit(solution)/shard_map/pallas_call | solution.py:289
  28.7 1.9 %copy.16 = bf16[2,256,512]{2,1,0:T(8,128)(2,1)} copy(bf16[2,256,512]{2,1,0:T(8,128)(2,1)} %get-tuple-element.7) | data formatting | bytes 1048576

commit v2 on v1

--- a/solution.py
+++ b/solution.py
@@ -61,6 +61,7 @@
     dec_in,
     own,
     other,
+    skill,
     load_sem,
     hs_sem,
     hr_sem,
@@ -72,7 +73,6 @@
     slots = links.shape[0]
     channels = w_dec.shape[0]
     points = vertex_map.shape[1]
-    padded = wdp.shape[0]
     me = lax.axis_index("node")
     mine = lax.axis_index("member")
     right = lax.rem(me + 1, shards)
@@ -210,44 +210,56 @@
             gathered = gathered + dot(planes[plane], onehot[...])
         return (gathered[0:channels] + prior[...].astype(F32)).astype(BF16)
 
+    ensemble = members * groups
+    skill_scale = 1.0 / ensemble
+    pull_scale = 1.0 / (ensemble * max(ensemble - 1, 1))
+
+    def unit(offset, scale):
+        inverse = lax.rsqrt(jnp.sum(offset * offset, axis=0, keepdims=True) + DIST_EPS)
+        return offset * (inverse * scale)
+
+    def points_loop(body):
+        def step(i, carry):
+            body(pl.ds(pl.multiple_of(i * LANES, LANES), LANES))
+            return carry
+
+        lax.fori_loop(0, points // LANES, step, 0, unroll=2)
+
     for m in range(members):
         own[m] = forecast([dec[m, plane] for plane in range(PLANES)])
-    for k, m, copy in dec_copies:
-        copy.wait_recv()
-        other[k * members + m] = forecast([dec_in[k, m, plane] for plane in range(PLANES)])
-
-    ensemble = members * groups
-
-    def unit(offset):
-        return offset * lax.rsqrt(jnp.sum(offset * offset, axis=0, keepdims=True) + DIST_EPS)
-
-    def points_step(step, carry):
-        cut = pl.ds(pl.multiple_of(step * LANES, LANES), LANES)
+
+    def own_terms(cut):
         anchors = [own[m, :, cut].astype(F32) for m in range(members)]
-        pulls = [None] * members
-
-        def add(m, value):
-            pulls[m] = value if pulls[m] is None else pulls[m] + value
-
+        truth = target[:, cut].astype(F32)
+        skills = [unit(anchor - truth, skill_scale) for anchor in anchors]
         for a in range(members):
             for b in range(a + 1, members):
-                pull = unit(anchors[a] - anchors[b])
-                add(a, pull)
-                add(b, -pull)
-        for b in range(other.shape[0]):
-            values = other[b, :, cut].astype(F32)
+                pull = unit(anchors[a] - anchors[b], pull_scale)
+                skills[a] = skills[a] - pull
+                skills[b] = skills[b] + pull
+        for a in range(members):
+            if dec_copies:
+                skill[a, :, cut] = skills[a]
+            else:
+                sens[a, :, cut] = (weights[:, cut] * skills[a]).astype(BF16)
+
+    points_loop(own_terms)
+
+    for i, (k, m, copy) in enumerate(dec_copies):
+        copy.wait_recv()
+        other[...] = forecast([dec_in[k, m, plane] for plane in range(PLANES)])
+
+        def other_terms(cut, last=i + 1 == len(dec_copies)):
+            values = other[:, cut].astype(F32)
             for a in range(members):
-                add(a, unit(anchors[a] - values))
-        truth = target[:, cut].astype(F32)
-        weight = weights[:, cut]
-        for a in range(members):
-            skill = unit(anchors[a] - truth) * (1.0 / ensemble)
-            if ensemble > 1:
-                skill = skill - pulls[a] * (1.0 / (ensemble * (ensemble - 1)))
-            sens[a, :, cut] = (weight * skill).astype(BF16)
-        return carry
-
-    lax.fori_loop(0, points // LANES, points_step, 0)
+                anchor = own[a, :, cut].astype(F32)
+                total = skill[a, :, cut] - unit(anchor - values, pull_scale)
+                if last:
+                    sens[a, :, cut] = (weights[:, cut] * total).astype(BF16)
+                else:
+                    skill[a, :, cut] = total
+
+        points_loop(other_terms)
 
     for m in range(members):
         node_grad = lax.dot_general(onehot[...], sens[m], NT, preferred_element_type=F32)
@@ -284,7 +296,7 @@
     points = target_vertex_map.shape[0]
     padded = -(-channels // 16) * 16
     vmem = pl.BlockSpec(memory_space=pltpu.VMEM)
-    hbm = pl.BlockSpec(memory_space=pl.ANY)
+    hbm = pl.BlockSpec(memory_space=pltpu.HBM)
     far = max(groups - 1, 1)
     return pl.pallas_call(
         functools.partial(kernel, groups, shards),
@@ -311,7 +323,8 @@
             pltpu.VMEM((members, PLANES, padded, rows), BF16),
             pltpu.VMEM((far, members, PLANES, padded, rows), BF16),
             pltpu.VMEM((members, channels, points), BF16),
-            pltpu.VMEM((far * members, channels, points), BF16),
+            pltpu.VMEM((channels, points), BF16),
+            pltpu.VMEM((members, channels, points), F32),
             pltpu.SemaphoreType.DMA((2 * layers + 2,)),
             pltpu.SemaphoreType.DMA((layers, members, 2)),
             pltpu.SemaphoreType.DMA((layers, members, 2)),
@@ -319,21 +332,21 @@
             pltpu.SemaphoreType.DMA((far, members)),
         ],
         compiler_params=pltpu.CompilerParams(
-            collective_id=0, has_side_effects=True, vmem_limit_bytes=62 * 1024 * 1024
+            collective_id=0, has_side_effects=True, vmem_limit_bytes=40 * 1024 * 1024
         ),
     )(
-        latent,
-        noise_draw,
-        mesh_links,
-        w_cond,
-        dec_gain.reshape(1, width),
-        w_dec,
-        target_vertex_map.reshape(1, points),
-        location_loss_factor.reshape(1, points),
-        w_in,
-        w_out,
-        prior_field,
-        target,
+        pltpu.with_memory_space_constraint(latent, pltpu.HBM),
+        pltpu.with_memory_space_constraint(noise_draw, pltpu.HBM),
+        pltpu.with_memory_space_constraint(mesh_links, pltpu.HBM),
+        pltpu.with_memory_space_constraint(w_cond, pltpu.HBM),
+        pltpu.with_memory_space_constraint(dec_gain.reshape(1, width), pltpu.HBM),
+        pltpu.with_memory_space_constraint(w_dec, pltpu.HBM),
+        pltpu.with_memory_space_constraint(target_vertex_map.reshape(1, points), pltpu.HBM),
+        pltpu.with_memory_space_constraint(location_loss_factor.reshape(1, points), pltpu.HBM),
+        pltpu.with_memory_space_constraint(w_in, pltpu.HBM),
+        pltpu.with_memory_space_constraint(w_out, pltpu.HBM),
+        pltpu.with_memory_space_constraint(prior_field, pltpu.HBM),
+        pltpu.with_memory_space_constraint(target, pltpu.HBM),
     )
 
 

time: 30.8 us -> 27.2 us (0.88)
  local copies, waits for them, and re-layouts: 3.93 us -> 1.87 us
  Pallas kernels: 26 us -> 24.6 us
    pallas_call x1, Pallas kernels: 26 us -> 24.6 us  [per_device(): pl.pallas_call(functools.partial(kernel, groups, shards), out_shape=(jax....]
    unnamed x1, local copies, waits for them, and re-layouts: 1.87 us -> 0.79 us
    pallas_call x1, local copies, waits for them, and re-layouts: 2.06 us -> 1.08 us  [per_device(): pl.pallas_call(functools.partial(kernel, groups, shards), out_shape=(jax....]
where the time goes in v2:
time: 27.2 us; the launch traced here: 27.1 us
  Pallas kernels  24.6 us (90%)
  local copies, waits for them, and re-layouts  1.87 us (7%)
  between operations  0.64 us (2%)
    pallas_call x1, Pallas kernels, per_device(): pl.pallas_call(functools.partial(kernel, groups, shards), out_shape=(jax....  24.6 us
    pallas_call x1, local copies, waits for them, and re-layouts, per_device(): pl.pallas_call(functools.partial(kernel, groups, shards), out_shape=(jax....  1.08 us
    unnamed x1, local copies, waits for them, and re-layouts  0.79 us

profile of v2, /device:TPU:0, one launch (start us, length us, event | category | flops | bytes accessed | tf_op | source)
XLA Modules:
  0.0 27.1 jit_solution(2680290711619792728)
XLA Ops:
  0.6 24.6 %shard_map.131 = (bf16[2,83,1024]{2,1,0:T(8,128)(2,1)S(1)}, bf16[2,256,512]{2,1,0:T(8,128)(2,1)S(1)}) custom-call(bf16[2,256,512]{2,1,0:T(8,128)(2,1)} %latent.1, f32[2,32]{1,0:T(2,128)} %noise.1, s32[6,256]{1,0:T(8,128)} %links.1, f32[2,32,512]{2,1,0:T(8,128)} %w_cond.1, f32[1,512]{1,0:T(1,128)} %bitcast.5, bf16[83,512]{1,0:T(8,128)(2,1)} %w_dec.1, ...), custom_call_target="tpu_custom_call" | custom-call | tf_op jit(solution)/shard_map/pallas_call | solution.py:301
  25.2 1.1 %copy.14 = bf16[2,83,1024]{2,0,1:T(2,128)(2,1)} copy(bf16[2,83,1024]{2,1,0:T(8,128)(2,1)S(1)} %get-tuple-element.2) | data formatting | bytes 679936 | tf_op jit(solution)/shard_map/pallas_call | solution.py:301
  26.3 0.8 %copy.16 = bf16[2,256,512]{2,1,0:T(8,128)(2,1)} copy(bf16[2,256,512]{2,1,0:T(8,128)(2,1)S(1)} %get-tuple-element.7) | data formatting | bytes 1048576

commit v3 on v2

--- a/solution.py
+++ b/solution.py
@@ -94,16 +94,15 @@
     for load in loads:
         load.start()
 
-    gains = [
-        1.0
-        + jnp.dot(
+    def gain_of(l):
+        return 1.0 + jnp.dot(
             noise[...],
             w_cond[l],
             precision=lax.Precision.HIGHEST,
             preferred_element_type=F32,
         )
-        for l in range(layers)
-    ]
+
+    gains = [gain_of(0)]
 
     halo_copies = {}
 
@@ -137,6 +136,7 @@
         if m == 0:
             pl.semaphore_wait(barrier, 2 + len(peers))
         send_halo(0, m)
+    gains += [gain_of(l) for l in range(1, layers)]
 
     total = rows * shards
     place = lax.rem(links[...] - (me * rows - WIN) + total, total)
@@ -157,11 +157,17 @@
         part[m] = dot(count_own[...], rows_bf)
         pre[m] = dot(rows_bf, wi[l, 0:width])
 
+    def forecast(planes):
+        gathered = dot(planes[0], onehot[...])
+        for plane in range(1, PLANES):
+            gathered = gathered + dot(planes[plane], onehot[...])
+        return (gathered[0:channels] + prior[...].astype(F32)).astype(BF16)
+
     dec_copies = []
+    loads[0].wait()
+    for m in range(members):
+        own_part(0, m)
     for l in range(layers):
-        loads[2 * l].wait()
-        for m in range(members):
-            own_part(l, m)
         if l == 0:
             local = vertex_map[...] - me * rows
             nodes = lax.broadcasted_iota(jnp.int32, (rows, points), 0)
@@ -169,6 +175,7 @@
             wdp[...] = jnp.zeros_like(wdp)
             wdp[0:channels] = w_dec[...]
         loads[2 * l + 1].wait()
+        loads[2 * l + 2].wait()
         for m in range(members):
             for copy in halo_copies[l, m]:
                 copy.wait_recv()
@@ -181,6 +188,7 @@
                 state[m] = values
                 normed[l + 1, m] = norm(values, gains[l + 1][m : m + 1])
                 send_halo(l + 1, m)
+                own_part(l + 1, m)
             else:
                 features = norm(values, dec_gain[...])
                 decoded = lax.dot_general(wdp[...], features, NT, preferred_element_type=F32)
@@ -200,15 +208,9 @@
                     )
                     copy.start()
                     dec_copies.append((k, m, copy))
-
-    for load in loads[2 * layers :]:
-        load.wait()
-
-    def forecast(planes):
-        gathered = dot(planes[0], onehot[...])
-        for plane in range(1, PLANES):
-            gathered = gathered + dot(planes[plane], onehot[...])
-        return (gathered[0:channels] + prior[...].astype(F32)).astype(BF16)
+                own[m] = forecast([dec[m, plane] for plane in range(PLANES)])
+
+    loads[2 * layers + 1].wait()
 
     ensemble = members * groups
     skill_scale = 1.0 / ensemble
@@ -224,9 +226,6 @@
             return carry
 
         lax.fori_loop(0, points // LANES, step, 0, unroll=2)
-
-    for m in range(members):
-        own[m] = forecast([dec[m, plane] for plane in range(PLANES)])
 
     def own_terms(cut):
         anchors = [own[m, :, cut].astype(F32) for m in range(members)]

time: 27.2 us -> 27.6 us (1.015)
  Pallas kernels: 24.6 us -> 24.9 us
    pallas_call x1, Pallas kernels: 24.6 us -> 24.9 us  [per_device(): pl.pallas_call(functools.partial(kernel, groups, shards), out_shape=(jax....]
where the time goes in v3:
time: 27.6 us; the launch traced here: 27.5 us
  Pallas kernels  24.9 us (90%)
  local copies, waits for them, and re-layouts  1.87 us (7%)
  between operations  0.64 us (2%)
    pallas_call x1, Pallas kernels, per_device(): pl.pallas_call(functools.partial(kernel, groups, shards), out_shape=(jax....  24.9 us
    pallas_call x1, local copies, waits for them, and re-layouts, per_device(): pl.pallas_call(functools.partial(kernel, groups, shards), out_shape=(jax....  1.08 us
    unnamed x1, local copies, waits for them, and re-layouts  0.79 us

profile of v3, /device:TPU:0, one launch (start us, length us, event | category | flops | bytes accessed | tf_op | source)
XLA Modules:
  0.0 27.5 jit_solution(1785292925151535374)
XLA Ops:
  0.6 24.9 %shard_map.131 = (bf16[2,83,1024]{2,1,0:T(8,128)(2,1)S(1)}, bf16[2,256,512]{2,1,0:T(8,128)(2,1)S(1)}) custom-call(bf16[2,256,512]{2,1,0:T(8,128)(2,1)} %latent.1, f32[2,32]{1,0:T(2,128)} %noise.1, s32[6,256]{1,0:T(8,128)} %links.1, f32[2,32,512]{2,1,0:T(8,128)} %w_cond.1, f32[1,512]{1,0:T(1,128)} %bitcast.5, bf16[83,512]{1,0:T(8,128)(2,1)} %w_dec.1, ...), custom_call_target="tpu_custom_call" | custom-call | tf_op jit(solution)/shard_map/pallas_call | solution.py:300
  25.6 1.1 %copy.14 = bf16[2,83,1024]{2,0,1:T(2,128)(2,1)} copy(bf16[2,83,1024]{2,1,0:T(8,128)(2,1)S(1)} %get-tuple-element.2) | data formatting | bytes 679936 | tf_op jit(solution)/shard_map/pallas_call | solution.py:300
  26.7 0.8 %copy.16 = bf16[2,256,512]{2,1,0:T(8,128)(2,1)} copy(bf16[2,256,512]{2,1,0:T(8,128)(2,1)S(1)} %get-tuple-element.7) | data formatting | bytes 1048576
